TPU v7x, 32 devices: a whole 2x2x4 slice. The times are simulated.
32 devices in a mesh: panel: 4 (over x, core), tile: 8 (over z, y).
Axes of the slice: x: 2, y: 2, z: 4, core: 2. Of those that a mesh axis runs over, the one named last changes fastest.
Arguments:
- residual: float32 [4, 8, 16, 8, 128], P('panel', 'tile'), may hold values from -6 to 6
- inverse: bfloat16 [4, 8, 2, 576, 576], P('panel', 'tile'), may hold values from -1 to 2
- blend_weight: float32 [576], replicated, may hold values from 0.1 to 1.9
- seam_table: int32 [4, 4, 3], replicated, may hold values from -1 to 3, as said below
Outputs:
- correction: float32 [4, 8, 16, 8, 128], P('panel', 'tile')
Inputs may be any that keep to these rules, and one draw needn't show every extreme that they name: seam_table[p, e] holds the neighbour panel across edge e of panel p (or -1), a rotation r and a reversal v. Every panel has neighbours across exactly two opposite edges (0 and 2, or 1 and 3) and the entries -1, 0, 0 on the other two; the panels form one closed cycle and each panel's two neighbours differ. If edge e of p faces panel q, then edge c = (e + 2 + r) mod 4 of q faces p with rotation (-r) mod 4 and the same reversal v. At least one seam joins edge 0 of a panel to edge 0 of another, with rotation 2 and reversal 1.
All inputs are finite; a program needn't handle non-finite values.
Results may differ from a plain program's by a relative error of at most 0.0029.
Values may be sent and summed in bfloat16 or wider, within the bound.
A program may use at most 128 MiB of HBM per device.

v0:
```python
import jax
import jax.numpy as jnp
from jax import lax
from jax.sharding import PartitionSpec as P

PANELS = 4
TILE_ROWS = 2
SUB = 8
INTERSECTION = 8


def passed_along(block, axis, distance):
    devices = range(lax.axis_size(axis))
    route = [(i - distance, i) for i in devices if i - distance in devices]
    return lax.ppermute(block, axis, route)


def neighbours_in(first_part, second_part, stride):
    from_below = passed_along(first_part, "tile", stride)
    from_above = passed_along(second_part, "tile", -stride)
    return (from_below, from_above)


def neighbours_out(first_part, second_part, stride):
    to_above = passed_along(first_part, "tile", stride)
    to_below = passed_along(second_part, "tile", -stride)
    return (to_above, to_below)


def band_index(edge_id, row_count, col_count):
    margin = INTERSECTION
    if edge_id == 0:
        return (slice(None), slice(0, margin))
    if edge_id == 1:
        return (slice(0, margin), slice(None))
    if edge_id == 2:
        return (slice(None), slice(col_count - margin, col_count))
    return (slice(row_count - margin, row_count), slice(None))


def to_band(window, edge_id):
    if edge_id == 0:
        return jnp.transpose(window[::-1], (1, 0, 2))
    if edge_id == 1:
        return window[::-1]
    if edge_id == 2:
        return jnp.transpose(window, (1, 0, 2))
    return window


def from_band(region, edge_id):
    if edge_id == 0:
        return jnp.transpose(region, (1, 0, 2))[::-1]
    if edge_id == 1:
        return region[::-1]
    if edge_id == 2:
        return jnp.transpose(region, (1, 0, 2))
    return region


def into_cells(edge_part, edge_id):
    if edge_id == 0:
        return jnp.transpose(edge_part, (1, 0, 2))
    if edge_id == 1:
        return edge_part
    if edge_id == 2:
        return jnp.transpose(edge_part[::-1], (1, 0, 2))
    return edge_part[::-1]


def placed(band, offset, live_edge, length_all):
    blank_band = jnp.zeros((band.shape[0], length_all, band.shape[2]), jnp.float32)
    filled = lax.dynamic_update_slice_in_dim(blank_band, band, offset, 1)
    return jnp.where(live_edge, filled, jnp.zeros_like(filled))


def build_buffer(bands, offsets, live_edge, panel_side, extra):
    length_all = panel_side + 2 * extra
    return jnp.stack(
        [
            (
                placed(bands[2 * slot_id], offsets[2 * slot_id], live_edge[2 * slot_id], length_all)
                + placed(
                    bands[2 * slot_id + 1],
                    offsets[2 * slot_id + 1],
                    live_edge[2 * slot_id + 1],
                    length_all,
                )
            )[:, extra : extra + panel_side]
            for slot_id in range(2)
        ]
    )


def slot_info(seam_row, slot_id):
    first_entry = seam_row[2 * slot_id]
    second_entry = seam_row[2 * slot_id + 1]
    first_live = first_entry[0] >= 0
    chosen = jnp.where(first_live, first_entry, second_entry)
    edge_id = jnp.where(first_live, 2 * slot_id, 2 * slot_id + 1)
    facing = (edge_id + 2 + chosen[1]) % 4
    return (jnp.maximum(chosen[0], 0), facing // 2, chosen[2])


def outgoing_of(totals, slot_facts):
    blank_slot = jnp.zeros_like(totals[0])
    return jnp.stack(
        [
            jnp.where(
                slot_facts[0][0] == target,
                totals[0],
                jnp.where(slot_facts[1][0] == target, totals[1], blank_slot),
            )
            for target in range(PANELS)
        ]
    )


def picked_of(arrived_all, slot_facts):
    return jnp.stack(
        [
            lax.dynamic_index_in_dim(arrived_all, slot_facts[slot_id][0], 0, keepdims=False)
            for slot_id in range(2)
        ]
    )


def gathered_edges(bands, seam_row, tile_rows, tile_cols):
    height = bands[0].shape[1]
    width = bands[1].shape[1]
    longest = max(height, width)
    columns = bands[0].shape[2]
    pieces = []
    for slot_id in range(2):
        column_type = seam_row[2 * slot_id, 0] >= 0
        column_band = bands[2 * slot_id]
        row_band = jnp.pad(bands[2 * slot_id + 1], ((0, 0), (0, longest - width), (0, 0)))
        pieces.append(jnp.where(column_type, column_band, row_band))
    gathered = lax.all_gather(jnp.stack(pieces)[None], "tile", axis=0, tiled=True)
    grid = gathered.reshape(tile_rows, tile_cols, 2, INTERSECTION, longest, columns)
    totals = []
    for slot_id in range(2):
        column_type = seam_row[2 * slot_id, 0] >= 0
        grid_col = 0 if slot_id == 0 else tile_cols - 1
        grid_row = 0 if slot_id == 0 else tile_rows - 1
        down_column = grid[:, grid_col, slot_id, :, :height]
        down_column = jnp.transpose(down_column, (1, 0, 2, 3)).reshape(
            INTERSECTION, tile_rows * height, columns
        )
        along_row = grid[grid_row, :, slot_id, :, :width]
        along_row = jnp.transpose(along_row, (1, 0, 2, 3)).reshape(
            INTERSECTION, tile_cols * width, columns
        )
        totals.append(jnp.where(column_type, down_column, along_row))
    return jnp.stack(totals)


def cross(bands, seam_row, forward, offsets, live_edge, panel_side, tile_rows, tile_cols):
    extra = 0 if forward else INTERSECTION
    slot_facts = [slot_info(seam_row, slot_id) for slot_id in range(2)]
    if forward:
        totals = gathered_edges(bands, seam_row, tile_rows, tile_cols)
        arrived_all = lax.all_to_all(
            outgoing_of(totals, slot_facts), "panel", split_axis=0, concat_axis=0, tiled=True
        )
    else:
        buffer = build_buffer(bands, offsets, live_edge, panel_side, extra)
        totals = lax.psum(buffer, "tile")
        arrived_all = lax.all_to_all(
            outgoing_of(totals, slot_facts), "panel", split_axis=0, concat_axis=0, tiled=True
        )
    arrived = picked_of(arrived_all, slot_facts)
    return [
        jnp.where(slot_facts[slot_id][2] > 0, arrived[slot_id][:, ::-1], arrived[slot_id])
        for slot_id in range(2)
    ]


def patches(padded, block_rows, block_cols):
    columns = padded.shape[-1]
    blocked = padded.reshape(block_rows + 2, SUB, block_cols + 2, SUB, columns)
    pieces = [
        blocked[row_shift : row_shift + block_rows, :, col_shift : col_shift + block_cols]
        for row_shift in range(3)
        for col_shift in range(3)
    ]
    stacked = jnp.stack(pieces).reshape(3, 3, block_rows, SUB, block_cols, SUB, columns)
    stacked = jnp.transpose(stacked, (2, 4, 0, 3, 1, 5, 6))
    return stacked.reshape(block_rows, block_cols, 9 * SUB * SUB, columns)


def intersection_add(solved, block_rows, block_cols):
    columns = solved.shape[-1]
    shaped = solved.reshape(block_rows, block_cols, 3, SUB, 3, SUB, columns)
    summed = jnp.zeros((block_rows + 2, SUB, block_cols + 2, SUB, columns), jnp.float32)
    for row_shift in range(3):
        for col_shift in range(3):
            block_part = jnp.transpose(shaped[:, :, row_shift, :, col_shift], (0, 2, 1, 3, 4))
            summed = summed.at[
                row_shift : row_shift + block_rows, :, col_shift : col_shift + block_cols
            ].add(block_part)
    return summed.reshape((block_rows + 2) * SUB, (block_cols + 2) * SUB, columns)


def local(residual, inverse, blend_weight, seam_table):
    margin = INTERSECTION
    source = residual[0, 0].astype(jnp.bfloat16)
    height, tile_width, columns = source.shape
    tile_rows = TILE_ROWS
    tile_cols = lax.axis_size("tile") // TILE_ROWS
    tile_id = lax.axis_index("tile")
    row_pos = tile_id // tile_cols
    col_pos = tile_id % tile_cols
    seam_row = lax.dynamic_index_in_dim(seam_table, lax.axis_index("panel"), 0, keepdims=False)
    panel_side = tile_width * tile_cols
    on_edge = [col_pos == 0, row_pos == 0, col_pos == tile_cols - 1, row_pos == tile_rows - 1]
    live_edge = [on_edge[edge_id] & (seam_row[edge_id, 0] >= 0) for edge_id in range(4)]
    offsets = [row_pos * height, col_pos * tile_width, row_pos * height, col_pos * tile_width]
    lengths = [height, tile_width, height, tile_width]
    left_valid = col_pos > 0
    right_valid = col_pos < tile_cols - 1
    below_rows, above_rows = neighbours_in(source[height - margin :], source[:margin], tile_cols)
    row_ext = jnp.concatenate([below_rows, source, above_rows], 0)
    left_cols, right_cols = neighbours_in(row_ext, row_ext, 1)
    left_cols = jnp.where(left_valid, left_cols, jnp.zeros_like(left_cols))
    right_cols = jnp.where(right_valid, right_cols, jnp.zeros_like(right_cols))
    extended = jnp.concatenate([left_cols, row_ext, right_cols], 1)
    own_strips = [
        jnp.transpose(source, (1, 0, 2)),
        source[:margin],
        jnp.transpose(source[:, ::-1], (1, 0, 2)),
        source[height - margin :][::-1],
    ]
    arrived = cross(
        own_strips, seam_row, True, offsets, live_edge, panel_side, tile_rows, tile_cols
    )
    rows_ext, cols_ext = (extended.shape[0], extended.shape[1])
    for edge_id in range(4):
        widened = jnp.pad(arrived[edge_id // 2], ((0, 0), (margin, margin), (0, 0)))
        window = lax.dynamic_slice_in_dim(
            widened, offsets[edge_id], lengths[edge_id] + 2 * margin, 1
        )
        where_band = band_index(edge_id, rows_ext, cols_ext)
        fresh_band = jnp.where(live_edge[edge_id], to_band(window, edge_id), extended[where_band])
        extended = extended.at[where_band].set(fresh_band)
    sub_rows, sub_cols = (height // SUB, tile_width // SUB)
    local_patches = patches(extended, sub_rows, sub_cols).reshape(
        sub_rows * sub_cols, 9 * SUB * SUB, columns
    )
    solved = jnp.einsum(
        "noi,nir->nor", inverse[0, 0], local_patches, preferred_element_type=jnp.float32
    )
    solved = solved * blend_weight[None, :, None]
    spread = intersection_add(
        solved.reshape(sub_rows, sub_cols, 9 * SUB * SUB, columns), sub_rows, sub_cols
    )
    ghost_sets = [
        from_band(spread[band_index(edge_id, rows_ext, cols_ext)], edge_id) for edge_id in range(4)
    ]
    returned = cross(
        ghost_sets, seam_row, False, offsets, live_edge, panel_side, tile_rows, tile_cols
    )
    got_left, got_right = neighbours_out(spread[:, tile_width + margin :], spread[:, :margin], 1)
    spread = spread.at[:, margin : 2 * margin].add(jnp.where(left_valid, got_left, 0.0))
    spread = spread.at[:, tile_width : tile_width + margin].add(
        jnp.where(right_valid, got_right, 0.0)
    )
    narrow = spread[:, margin : tile_width + margin]
    got_below, got_above = neighbours_out(narrow[height + margin :], narrow[:margin], tile_cols)
    narrow = narrow.at[margin : 2 * margin].add(got_below)
    narrow = narrow.at[height : height + margin].add(got_above)
    owned_cells = narrow[margin : height + margin]
    for edge_id in range(4):
        edge_part = lax.dynamic_slice_in_dim(
            returned[edge_id // 2], offsets[edge_id], lengths[edge_id], 1
        )
        where_cells = band_index(edge_id, height, tile_width)
        addition = jnp.where(live_edge[edge_id], into_cells(edge_part, edge_id), 0.0)
        owned_cells = owned_cells.at[where_cells].add(addition)
    return owned_cells[None, None]


def solution(mesh):
    placed = (P("panel", "tile", None, None, None), P("panel", "tile", None, None, None), P(), P())
    return jax.shard_map(
        local,
        mesh=mesh,
        in_specs=placed,
        out_specs=P("panel", "tile", None, None, None),
        check_vma=False,
    )
```

profile of v0, /device:TPU:0, one launch (start us, length us, event | category | flops | bytes accessed | tf_op | source)
XLA Modules:
  0.0 179.4 jit_solution(4141283619340578663)
XLA Ops:
  6.5 1.0 convert_element_type.14
  7.5 1.3 collective-permute-start.1
  8.8 6.0 %collective-permute-start = (bf16[8,8,128]{2,1,0:T(8,128)(2,1)S(1)}, bf16[8,8,128]{2,1,0:T(8,128)(2,1)S(1)}, u32[]{:S(2)}, u32[]{:S(2)}) collective-permute-start(bf16[8,8,128]{2,1,0:T(8,128)(2,1)S(1)} %get-tuple-element.301), channel_id=1, source_target_pairs={{0,4},{1,5},{2,6},{3,7},{8,12},{9,13},{10,14},{11,15},{16,20},{17,... | collective-permute-start | bytes 49160 | tf_op jit(solution)/shard_map/ppermute | solution.py:15
  14.8 0.8 convert_bitcast_fusion.1
  15.6 0.8 convert_bitcast_fusion
  19.3 31.4 %all-gather = bf16[16,8,16,128]{3,2,1,0:T(8,128)(2,1)S(1)} all-gather(bf16[2,8,16,128]{3,2,1,0:T(8,128)(2,1)S(1)} %pad_maximum_fusion.5), channel_id=2, replica_groups=mesh['panel'=4,'tile'=8] {'tile'}, dimensions={0}, use_global_device_ids=true | all-gather | bytes 589824 | tf_op jit(solution)/shard_map/all_gather | solution.py:139
  55.5 3.6 %all-to-all-start = ((bf16[4,8,32,128]{3,2,1,0:T(8,128)(2,1)}), bf16[4,8,32,128]{3,2,1,0:T(8,128)(2,1)S(1)}, u32[]{:S(2)}, u32[]{:S(2)}) async-start(bf16[4,8,32,128]{3,2,1,0:T(8,128)(2,1)} %pad_maximum_fusion.1), calls=%async_computation | async-start | bytes 524288 | tf_op jit(solution)/shard_map/all_to_all | solution.py:163
  62.9 1.3 concatenate.55
  65.0 1.3 collective-permute-start.3
  66.9 4.5 %collective-permute-start.2 = (bf16[32,8,128]{2,1,0:T(8,128)(2,1)S(1)}, bf16[32,8,128]{2,1,0:T(8,128)(2,1)S(1)}, u32[]{:S(2)}, u32[]{:S(2)}) collective-permute-start(bf16[32,8,128]{2,1,0:T(8,128)(2,1)S(1)} %pad_maximum_fusion.4), channel_id=1, source_target_pairs={{0,1},{1,2},{2,3},{3,4},{4,5},{5,6},{6,7},{8,9},{9,10},{10,11},{11... | collective-permute-start | bytes 196616 | tf_op jit(solution)/shard_map/ppermute | solution.py:15
  71.5 1.9 %collective-permute-done.2 = bf16[32,8,128]{2,1,0:T(8,128)(2,1)S(1)} collective-permute-done((bf16[32,8,128]{2,1,0:T(8,128)(2,1)S(1)}, bf16[32,8,128]{2,1,0:T(8,128)(2,1)S(1)}, u32[]{:S(2)}, u32[]{:S(2)}) %collective-permute-start.2) | collective-permute-done | bytes 65568 | tf_op jit(solution)/shard_map/ppermute | solution.py:15
  74.8 1.3 fusion.7
  76.1 1.8 %fusion.8 = f32[4,8,3,8,128]{4,3,1,0,2:T(8,128)S(1)} fusion(f32[4,8,3,8,128]{4,3,1,0,2:T(8,128)S(1)} %fusion.7, s32[]{:T(128)} %bitcast.56, s32[]{:T(128)} %bitcast.57, f32[2,1,3,8,3,8,128]{6,5,4,3,2,0,1:T(8,128)S(1)} %bitcast.226, pred[]{:T(512)} %get-tuple-element.273), kind=kLoop, calls=%fused_computation.33 | loop fusion | flops 32768 | bytes 196617 | tf_op jit(solution)/shard_map/scatter-add | solution.py:201
  78.2 1.3 collective-permute-start.5
  79.5 4.9 %collective-permute-start.4 = (f32[32,8,128]{2,1,0:T(8,128)S(1)}, f32[32,8,128]{2,1,0:T(8,128)S(1)}, u32[]{:S(2)}, u32[]{:S(2)}) collective-permute-start(f32[32,8,128]{2,1,0:T(8,128)S(1)} %get-tuple-element.289), channel_id=1, source_target_pairs={{0,1},{1,2},{2,3},{3,4},{4,5},{5,6},{6,7},{8,9},{9,10},{10,11},{11... | collective-permute-start | bytes 393224 | tf_op jit(solution)/shard_map/ppermute | solution.py:15
  85.4 2.7 %collective-permute-done.4 = f32[32,8,128]{2,1,0:T(8,128)S(1)} collective-permute-done((f32[32,8,128]{2,1,0:T(8,128)S(1)}, f32[32,8,128]{2,1,0:T(8,128)S(1)}, u32[]{:S(2)}, u32[]{:S(2)}) %collective-permute-start.4) | collective-permute-done | bytes 131104 | tf_op jit(solution)/shard_map/ppermute | solution.py:15
  88.2 4.1 %collective-permute-start.6 = (f32[8,8,128]{2,1,0:T(8,128)S(1)}, f32[8,8,128]{2,1,0:T(8,128)S(1)}, u32[]{:S(2)}, u32[]{:S(2)}) collective-permute-start(f32[8,8,128]{2,1,0:T(8,128)S(1)} %slice.940), channel_id=1, source_target_pairs={{0,4},{1,5},{2,6},{3,7},{8,12},{9,13},{10,14},{11,15},{16,20},{17,... | collective-permute-start | bytes 98312 | tf_op jit(solution)/shard_map/ppermute | solution.py:15
  92.2 64.6 %all-reduce.7.cloned.1.call-done = f32[2,8,32,128]{3,2,1,0:T(8,128)} async-done(((f32[2,8,32,128]{3,2,1,0:T(8,128)}), f32[2,8,32,128]{3,2,1,0:T(8,128)}) %all-reduce.7.cloned.1.call-update) | async-done | bytes 262160 | tf_op jit(solution)/shard_map/psum | solution.py:168
  156.9 1.0 select_select_fusion.3
  157.9 0.9 pad_maximum_fusion
  158.7 3.5 %all-to-all-start.1 = ((f32[4,8,32,128]{3,2,1,0:T(8,128)}), f32[4,8,32,128]{3,2,1,0:T(8,128)S(1)}, u32[]{:S(2)}, u32[]{:S(2)}) async-start(f32[4,8,32,128]{3,2,1,0:T(8,128)} %pad_maximum_fusion), calls=%async_computation.1 | async-start | bytes 1048576 | tf_op jit(solution)/shard_map/all_to_all | solution.py:169
  162.3 1.3 collective-permute-start.7
  163.6 6.0 %collective-permute-done.7 = f32[8,8,128]{2,1,0:T(8,128)S(1)} collective-permute-done((f32[8,8,128]{2,1,0:T(8,128)S(1)}, f32[8,8,128]{2,1,0:T(8,128)S(1)}, u32[]{:S(2)}, u32[]{:S(2)}) %collective-permute-start.7) | collective-permute-done | bytes 32800 | tf_op jit(solution)/shard_map/ppermute | solution.py:15
  169.6 1.4 all-to-all-done.1
  (111 shorter events, 10.2 us)
Async XLA Ops:
  6.5 67.5 %copy-start = (bf16[1,1,2,576,576]{4,3,2,1,0:T(8,128)(2,1)S(1)}, bf16[1,1,2,576,576]{4,3,2,1,0:T(8,128)(2,1)}, u32[]{:S(2)}) copy-start(bf16[1,1,2,576,576]{4,3,2,1,0:T(8,128)(2,1)} %param.51) | copy-start | bytes 3981316
  6.5 44.2 %copy-start.1 = (s32[4,4,3]{1,0,2:T(4,128)S(1)}, s32[4,4,3]{1,0,2:T(4,128)}, u32[]{:S(2)}) copy-start(s32[4,4,3]{1,0,2:T(4,128)} %param.53) | copy-start | bytes 580
  7.5 57.4 %collective-permute-start.1 = (bf16[8,8,128]{2,1,0:T(8,128)(2,1)S(1)}, bf16[8,8,128]{2,1,0:T(8,128)(2,1)S(1)}, u32[]{:S(2)}, u32[]{:S(2)}) collective-permute-start(bf16[8,8,128]{2,1,0:T(8,128)(2,1)S(1)} %get-tuple-element.302), channel_id=1, source_target_pairs={{4,0},{5,1},{6,2},{7,3},{12,8},{13,9},{14,10},{15,11},{20,16},{21,... | collective-permute-start | bytes 49160 | tf_op jit(solution)/shard_map/ppermute | solution.py:15
  8.8 56.2 %collective-permute-start = (bf16[8,8,128]{2,1,0:T(8,128)(2,1)S(1)}, bf16[8,8,128]{2,1,0:T(8,128)(2,1)S(1)}, u32[]{:S(2)}, u32[]{:S(2)}) collective-permute-start(bf16[8,8,128]{2,1,0:T(8,128)(2,1)S(1)} %get-tuple-element.301), channel_id=1, source_target_pairs={{0,4},{1,5},{2,6},{3,7},{8,12},{9,13},{10,14},{11,15},{16,20},{17,... | collective-permute-start | bytes 49160 | tf_op jit(solution)/shard_map/ppermute | solution.py:15
  50.7 15.6 %copy-start.3 = (s32[5]{0:T(128)S(1)}, s32[5]{0:T(128)}, u32[]{:S(2)}) copy-start(s32[5]{0:T(128)} %constant.662.clone.1) | copy-start | bytes 64
  55.5 18.0 %all-to-all-start = ((bf16[4,8,32,128]{3,2,1,0:T(8,128)(2,1)}), bf16[4,8,32,128]{3,2,1,0:T(8,128)(2,1)S(1)}, u32[]{:S(2)}, u32[]{:S(2)}) async-start(bf16[4,8,32,128]{3,2,1,0:T(8,128)(2,1)} %pad_maximum_fusion.1), calls=%async_computation | async-start | bytes 524288 | tf_op jit(solution)/shard_map/all_to_all | solution.py:163
  59.1 97.7 %all-reduce.7.cloned.1.call-start = ((), (), s32[]{:S(2)}) async-start(), calls=%async_computation.2 | async-start | bytes 524288 | tf_op jit(solution)/shard_map/psum | solution.py:168
  65.0 6.5 %collective-permute-start.3 = (bf16[32,8,128]{2,1,0:T(8,128)(2,1)S(1)}, bf16[32,8,128]{2,1,0:T(8,128)(2,1)S(1)}, u32[]{:S(2)}, u32[]{:S(2)}) collective-permute-start(bf16[32,8,128]{2,1,0:T(8,128)(2,1)S(1)} %pad_maximum_fusion.4), channel_id=1, source_target_pairs={{1,0},{2,1},{3,2},{4,3},{5,4},{6,5},{7,6},{9,8},{10,9},{11,10},{12... | collective-permute-start | bytes 196616 | tf_op jit(solution)/shard_map/ppermute | solution.py:15
  66.9 6.4 %collective-permute-start.2 = (bf16[32,8,128]{2,1,0:T(8,128)(2,1)S(1)}, bf16[32,8,128]{2,1,0:T(8,128)(2,1)S(1)}, u32[]{:S(2)}, u32[]{:S(2)}) collective-permute-start(bf16[32,8,128]{2,1,0:T(8,128)(2,1)S(1)} %pad_maximum_fusion.4), channel_id=1, source_target_pairs={{0,1},{1,2},{2,3},{3,4},{4,5},{5,6},{6,7},{8,9},{9,10},{10,11},{11... | collective-permute-start | bytes 196616 | tf_op jit(solution)/shard_map/ppermute | solution.py:15
  73.5 0.7 copy-start.2
  78.2 7.2 %collective-permute-start.5 = (f32[32,8,128]{2,1,0:T(8,128)S(1)}, f32[32,8,128]{2,1,0:T(8,128)S(1)}, u32[]{:S(2)}, u32[]{:S(2)}) collective-permute-start(f32[32,8,128]{2,1,0:T(8,128)S(1)} %get-tuple-element.288), channel_id=1, source_target_pairs={{1,0},{2,1},{3,2},{4,3},{5,4},{6,5},{7,6},{9,8},{10,9},{11,10},{12... | collective-permute-start | bytes 393224 | tf_op jit(solution)/shard_map/ppermute | solution.py:15
  79.5 8.7 %collective-permute-start.4 = (f32[32,8,128]{2,1,0:T(8,128)S(1)}, f32[32,8,128]{2,1,0:T(8,128)S(1)}, u32[]{:S(2)}, u32[]{:S(2)}) collective-permute-start(f32[32,8,128]{2,1,0:T(8,128)S(1)} %get-tuple-element.289), channel_id=1, source_target_pairs={{0,1},{1,2},{2,3},{3,4},{4,5},{5,6},{6,7},{8,9},{9,10},{10,11},{11... | collective-permute-start | bytes 393224 | tf_op jit(solution)/shard_map/ppermute | solution.py:15
  88.2 74.1 %collective-permute-start.6 = (f32[8,8,128]{2,1,0:T(8,128)S(1)}, f32[8,8,128]{2,1,0:T(8,128)S(1)}, u32[]{:S(2)}, u32[]{:S(2)}) collective-permute-start(f32[8,8,128]{2,1,0:T(8,128)S(1)} %slice.940), channel_id=1, source_target_pairs={{0,4},{1,5},{2,6},{3,7},{8,12},{9,13},{10,14},{11,15},{16,20},{17,... | collective-permute-start | bytes 98312 | tf_op jit(solution)/shard_map/ppermute | solution.py:15
  158.7 12.3 %all-to-all-start.1 = ((f32[4,8,32,128]{3,2,1,0:T(8,128)}), f32[4,8,32,128]{3,2,1,0:T(8,128)S(1)}, u32[]{:S(2)}, u32[]{:S(2)}) async-start(f32[4,8,32,128]{3,2,1,0:T(8,128)} %pad_maximum_fusion), calls=%async_computation.1 | async-start | bytes 1048576 | tf_op jit(solution)/shard_map/all_to_all | solution.py:169
  162.3 7.3 %collective-permute-start.7 = (f32[8,8,128]{2,1,0:T(8,128)S(1)}, f32[8,8,128]{2,1,0:T(8,128)S(1)}, u32[]{:S(2)}, u32[]{:S(2)}) collective-permute-start(f32[8,8,128]{2,1,0:T(8,128)S(1)} %get-tuple-element.296), channel_id=1, source_target_pairs={{4,0},{5,1},{6,2},{7,3},{12,8},{13,9},{14,10},{15,11},{20,16},{21,... | collective-permute-start | bytes 98312 | tf_op jit(solution)/shard_map/ppermute | solution.py:15
Sparse Core Ops, SparseCore 0:
  85.5 71.2 all-reduce.6
where the time goes:
time: 180 us; the launch traced here: 179 us
  waiting for transfers between devices  76.6 us (43%)
  starting transfers between devices  31.7 us (18%)
  blocking collectives  31.4 us (17%)
  between operations  20.5 us (11%)
  other arithmetic  11.2 us (6%)
  local copies, waits for them, and re-layouts  7.37 us (4%)
    psum x1, waiting for transfers between devices, cross(): totals = lax.psum(buffer, 'tile')  64.6 us
    all_gather x1, blocking collectives, gathered_edges(): lax.all_gather(jnp.stack(pieces)[None], 'tile', axis=0, tiled=True)  31.4 us
    ppermute x8, starting transfers between devices, passed_along(): return lax.ppermute(block, axis, route)  24.6 us
    ppermute x8, waiting for transfers between devices, passed_along(): return lax.ppermute(block, axis, route)  10.6 us
    all_to_all x2, starting transfers between devices, cross(): lax.all_to_all(outgoing_of(totals, slot_facts), 'panel', split_axis=0, co...  7.11 us
  transfers between devices with their start and end apart: 11, of which 5 were waited for; matrix products, arithmetic and copies ran while one was open for 7% of the time, Pallas kernels for 0%

commit v1 on v0

v1 whole, which is shorter than its diff:
```python
import functools

import jax
import jax.numpy as jnp
from jax import lax
from jax.experimental import pallas as pl
from jax.experimental.pallas import tpu as pltpu
from jax.sharding import PartitionSpec as P

TILE_ROWS = 2
SUB = 8
CELL = SUB * SUB
MESH = pl.DeviceIdType.MESH
SLOTS = 4
UNROLLED = 8
BF = jnp.bfloat16
F32 = jnp.float32


def repeat(count, body):
    if count <= UNROLLED:
        for step in range(count):
            body(step)
    else:
        pl.loop(0, count)(body)


def wrapped(index, size):
    return lax.rem(index + size, size)


def pick(options, index):
    out = options[-1]
    for place in range(len(options) - 2, -1, -1):
        out = jnp.where(index == place, options[place], out)
    return out


def kernel(
    panels, tiles, sub_rows,
    seam, residual, inverse, blend, out,
    held, shared, window_out, window_in, ghost_out, ghost_in, part_out, part_in,
    ext, spread, weight, inv_sem,
    tile_send, tile_recv, win_send, win_recv, gho_send, gho_recv, par_send, par_recv,
):
    cols = tiles // TILE_ROWS
    side = cols
    depth = sub_rows + 2
    panel, tile = lax.axis_index("panel"), lax.axis_index("tile")
    row, col = lax.div(tile, cols), lax.rem(tile, cols)

    def on_edge(edge, at_row, at_col):
        return pick([at_col == 0, at_row == 0, at_col == cols - 1, at_row == TILE_ROWS - 1], edge)

    def live_edge(of_panel, at_row, at_col):
        edge, found = jnp.int32(0), jnp.int32(0)
        for e in range(4):
            here = on_edge(e, at_row, at_col) & (seam[of_panel, e, 0] >= 0)
            edge = jnp.where(here, e, edge)
            found = jnp.where(here, 1, found)
        return edge, found

    def window_start(edge):
        return jnp.where(lax.rem(edge, 2) == 0, row * sub_rows, col) - 1

    def window_length(edge):
        return jnp.where(lax.rem(edge, 2) == 0, depth, 3)

    barrier = pltpu.get_barrier_semaphore()

    def greet_tile(step):
        pl.semaphore_signal(
            barrier, inc=1, device_id=(panel, wrapped(tile + step + 1, tiles)), device_id_type=MESH
        )

    repeat(tiles - 1, greet_tile)
    for off in range(1, panels):
        pl.semaphore_signal(
            barrier, inc=1, device_id=(wrapped(panel + off, panels), tile), device_id_type=MESH
        )

    def load_inverse(n):
        slot = lax.rem(n, SLOTS) if not isinstance(n, int) else n % SLOTS
        return pltpu.make_async_copy(inverse.at[n], held.at[slot], inv_sem.at[slot])

    for n in range(min(sub_rows, SLOTS)):
        load_inverse(n).start()

    def own_blocks(j):
        block = residual[pl.ds(j * SUB, SUB)].reshape(CELL, -1)
        shared[tile, j] = block.astype(BF)

    repeat(sub_rows, own_blocks)
    window_in[panel] = jnp.zeros(window_in.shape[1:], BF)
    ghost_in[panel] = jnp.zeros(ghost_in.shape[1:], BF)
    pl.semaphore_wait(barrier, tiles - 1 + panels - 1)

    def tile_copy(step, slot, target):
        return pltpu.make_async_remote_copy(
            src_ref=shared.at[slot], dst_ref=shared.at[slot],
            send_sem=tile_send.at[step], recv_sem=tile_recv.at[slot],
            device_id=(panel, target), device_id_type=MESH,
        )

    repeat(tiles - 1, lambda s: tile_copy(s, tile, wrapped(tile + s + 1, tiles)).start())

    lanes = residual.shape[-1]
    weight[...] = jnp.transpose(jnp.broadcast_to(blend[...], (lanes, blend.shape[1])))
    edge, found = live_edge(panel, row, col)
    neighbour = jnp.maximum(seam[panel, edge, 0], 0)
    facing = lax.rem(edge + 2 + seam[panel, edge, 1], 4)
    reverse = seam[panel, edge, 2]

    def source_cell(ghost):
        i, j = lax.shift_right_logical(ghost, 3), ghost & (SUB - 1)
        d = pick([SUB - 1 - j, SUB - 1 - i, j, i], edge)
        s = jnp.where(lax.rem(edge, 2) == 0, i, j)
        s = jnp.where(reverse > 0, SUB - 1 - s, s)
        across = jnp.where(facing >= 2, SUB - 1 - d, d)
        return jnp.where(lax.rem(facing, 2) == 0, s * SUB + across, across * SUB + s)

    shape = (CELL, CELL)
    first, second = lax.broadcasted_iota(jnp.int32, shape, 0), lax.broadcasted_iota(jnp.int32, shape, 1)
    turn = jnp.where((source_cell(first) == second) & (found > 0), 1.0, 0.0).astype(BF)
    turn_back = jnp.where((source_cell(second) == first) & (found > 0), 1.0, 0.0).astype(BF)

    def tile_arrival(step):
        source = wrapped(tile - step - 1, tiles)
        tile_copy(step, source, source).wait_recv()

    repeat(tiles - 1, tile_arrival)

    def window_copy(off, slot, target):
        return pltpu.make_async_remote_copy(
            src_ref=window_out.at[off - 1], dst_ref=window_in.at[slot],
            send_sem=win_send.at[off - 1], recv_sem=win_recv.at[slot],
            device_id=(target, tile), device_id_type=MESH,
        )

    for off in range(1, panels):
        other = wrapped(panel + off, panels)
        its_edge, its_found = live_edge(other, row, col)
        ours = (its_found > 0) & (seam[other, its_edge, 0] == panel)
        my_edge = lax.rem(its_edge + 2 + seam[other, its_edge, 1], 4)
        flip = seam[other, its_edge, 2]
        start, length = window_start(its_edge), window_length(its_edge)

        def fill(k, off=off, ours=ours, my_edge=my_edge, flip=flip, start=start, length=length):
            b = start + k
            good = ours & (b >= 0) & (b < side) & (k < length)
            b = jnp.where(flip > 0, side - 1 - b, b)
            b = jnp.clip(b, 0, side - 1)
            at_row = pick([b, 0, b, side - 1], my_edge)
            at_col = pick([0, b, cols - 1, b], my_edge)
            block = shared[lax.div(at_row, sub_rows) * cols + at_col, lax.rem(at_row, sub_rows)]
            window_out[off - 1, k] = jnp.where(good, block, jnp.zeros_like(block))

        repeat(depth, fill)
        window_copy(off, panel, other).start()

    def inner(ri):
        for ci in range(3):
            at_row, at_col = row * sub_rows + ri - 1, col + ci - 1
            inside = (at_row >= 0) & (at_row < side) & (at_col >= 0) & (at_col < cols)
            at_row, at_col = jnp.clip(at_row, 0, side - 1), jnp.clip(at_col, 0, cols - 1)
            block = shared[lax.div(at_row, sub_rows) * cols + at_col, lax.rem(at_row, sub_rows)]
            block = block.astype(F32)
            block = jnp.where(inside, block, jnp.zeros_like(block))
            ext[ri, :, ci] = block.reshape(SUB, SUB, lanes)

    repeat(depth, inner)

    for off in range(1, panels):
        source = wrapped(panel - off, panels)
        window_copy(off, source, source).wait_recv()

    def outer_side(k):
        block = jnp.dot(turn, window_in[neighbour, k], preferred_element_type=F32)
        block = block.reshape(SUB, SUB, lanes)
        for e, (ri, ci) in enumerate(((k, 0), (0, k), (k, 2), (depth - 1, k))):
            if e % 2 == 1 and not (isinstance(k, int) and k < 3):
                continue
            ext[ri, :, ci] += jnp.where(edge == e, block, jnp.zeros_like(block))

    for k in range(3):
        outer_side(k)
    if depth > 3:
        repeat_from = depth - 3
        repeat(repeat_from, lambda k: outer_side(jnp.int32(k) + 3 if isinstance(k, int) else k + 3))

    spread[...] = jnp.zeros_like(spread)

    def solve(n):
        load_inverse(n).wait()
        slot = n % SLOTS if isinstance(n, int) else lax.rem(n, SLOTS)
        patch = ext[pl.ds(n, 3)].reshape(9 * CELL, lanes).astype(BF)
        solved = jnp.dot(held[slot], patch, preferred_element_type=F32) * weight[...]
        spread[pl.ds(n, 3)] += solved.reshape(3, SUB, 3, SUB, lanes)
        if sub_rows > SLOTS:
            @pl.when(n + SLOTS < sub_rows)
            def _():
                load_inverse(n + SLOTS).start()

    repeat(sub_rows, solve)

    def ghost_copy(off, slot, target):
        return pltpu.make_async_remote_copy(
            src_ref=ghost_out, dst_ref=ghost_in.at[slot],
            send_sem=gho_send.at[off - 1], recv_sem=gho_recv.at[slot],
            device_id=(target, tile), device_id_type=MESH,
        )

    def ghost(k):
        even = lax.rem(edge, 2) == 0
        ri = jnp.where(even, k, jnp.where(edge == 1, 0, depth - 1))
        ci = jnp.where(even, edge, jnp.minimum(k, 2))
        raw = spread[ri, :, ci].reshape(CELL, lanes).astype(BF)
        ghost_out[k] = jnp.dot(turn_back, raw, preferred_element_type=F32).astype(BF)

    repeat(depth, ghost)
    for off in range(1, panels):
        ghost_copy(off, panel, wrapped(panel + off, panels)).start()
    for off in range(1, panels):
        source = wrapped(panel - off, panels)
        ghost_copy(off, source, source).wait_recv()

    def part(target, j):
        at_row, at_col = lax.div(target, cols), lax.rem(target, cols)
        ri, ci = (at_row - row) * sub_rows + j + 1, at_col - col + 1
        near = (ri >= 0) & (ri < depth) & (ci >= 0) & (ci < 3)
        block = spread[jnp.clip(ri, 0, depth - 1), :, jnp.clip(ci, 0, 2)].reshape(CELL, lanes)
        block = jnp.where(near, block, jnp.zeros_like(block))
        its_edge, its_found = live_edge(panel, at_row, at_col)
        other = jnp.maximum(seam[panel, its_edge, 0], 0)
        far_edge = lax.rem(its_edge + 2 + seam[panel, its_edge, 1], 4)
        even = lax.rem(its_edge, 2) == 0
        b = jnp.where(even, at_row * sub_rows + j, at_col)
        good = (its_found > 0) & on_edge(far_edge, row, col)
        good = good & (even | (j == jnp.where(its_edge == 1, 0, sub_rows - 1)))
        b = jnp.where(seam[panel, its_edge, 2] > 0, side - 1 - b, b)
        k = b - window_start(far_edge)
        good = good & (k >= 0) & (k < window_length(far_edge))
        seam_block = ghost_in[other, jnp.clip(k, 0, depth - 1)].astype(F32)
        return block + jnp.where(good, seam_block, jnp.zeros_like(seam_block))

    def part_copy(step, slot, target):
        return pltpu.make_async_remote_copy(
            src_ref=part_out.at[step], dst_ref=part_in.at[slot],
            send_sem=par_send.at[step], recv_sem=par_recv.at[slot],
            device_id=(panel, target), device_id_type=MESH,
        )

    def send_part(step):
        target = wrapped(tile + step + 1, tiles)

        def one(j):
            part_out[step, j] = part(target, j).astype(BF)

        repeat(sub_rows, one)
        part_copy(step, tile, target).start()

    repeat(tiles - 1, send_part)

    def own_part(j):
        out[pl.ds(j * SUB, SUB)] = part(tile, j).reshape(SUB, SUB, lanes)

    repeat(sub_rows, own_part)

    def take_part(step):
        source = wrapped(tile - step - 1, tiles)
        part_copy(step, source, source).wait_recv()

        def one(j):
            here = pl.ds(j * SUB, SUB)
            out[here] += part_in[source, j].astype(F32).reshape(SUB, SUB, lanes)

        repeat(sub_rows, one)

    repeat(tiles - 1, take_part)

    def sent(step):
        tile_copy(step, tile, wrapped(tile + step + 1, tiles)).wait_send()
        part_copy(step, tile, wrapped(tile + step + 1, tiles)).wait_send()

    repeat(tiles - 1, sent)
    for off in range(1, panels):
        window_copy(off, panel, wrapped(panel + off, panels)).wait_send()
        ghost_copy(off, panel, wrapped(panel + off, panels)).wait_send()


def local(panels, tiles, residual, inverse, blend_weight, seam_table):
    height, width, lanes = residual.shape[2:]
    sub_rows = height // SUB
    depth = sub_rows + 2
    cells = blend_weight.shape[0]
    vmem = pl.BlockSpec(memory_space=pltpu.VMEM)
    sem = pltpu.SemaphoreType.DMA
    block = (CELL, lanes)
    out = pl.pallas_call(
        functools.partial(kernel, panels, tiles, sub_rows),
        out_shape=jax.ShapeDtypeStruct((height, width, lanes), F32),
        in_specs=[
            pl.BlockSpec(memory_space=pltpu.SMEM), vmem, pl.BlockSpec(memory_space=pl.ANY), vmem,
        ],
        out_specs=vmem,
        scratch_shapes=[
            pltpu.VMEM((min(sub_rows, SLOTS), cells, cells), BF),
            pltpu.VMEM((tiles, sub_rows) + block, BF),
            pltpu.VMEM((panels - 1, depth) + block, BF),
            pltpu.VMEM((panels, depth) + block, BF),
            pltpu.VMEM((depth,) + block, BF),
            pltpu.VMEM((panels, depth) + block, BF),
            pltpu.VMEM((tiles - 1, sub_rows) + block, BF),
            pltpu.VMEM((tiles, sub_rows) + block, BF),
            pltpu.VMEM((depth, SUB, 3, SUB, lanes), F32),
            pltpu.VMEM((depth, SUB, 3, SUB, lanes), F32),
            pltpu.VMEM((cells, lanes), F32),
            sem((min(sub_rows, SLOTS),)),
            sem((tiles - 1,)), sem((tiles,)),
            sem((panels - 1,)), sem((panels,)),
            sem((panels - 1,)), sem((panels,)),
            sem((tiles - 1,)), sem((tiles,)),
        ],
        compiler_params=pltpu.CompilerParams(
            collective_id=0, has_side_effects=True, vmem_limit_bytes=67043328
        ),
    )(seam_table, residual[0, 0], inverse[0, 0], blend_weight[None])
    return out[None, None]


def solution(mesh):
    spec = P("panel", "tile", None, None, None)
    sizes = dict(mesh.shape)
    return jax.shard_map(
        functools.partial(local, sizes["panel"], sizes["tile"]),
        mesh=mesh,
        in_specs=(spec, spec, P(), P()),
        out_specs=spec,
        check_vma=False,
    )
```

time: 180 us -> 33.8 us (0.19)
  waiting for transfers between devices: 76.6 us -> 0 us
  starting transfers between devices: 31.7 us -> 0 us
  blocking collectives: 31.4 us -> 0 us
  Pallas kernels: 0 us -> 29.2 us
  between operations: 20.5 us -> 0.01 us
  other arithmetic: 11.2 us -> 0 us
  local copies, waits for them, and re-layouts: 7.37 us -> 4.11 us
    psum x1 -> x0, waiting for transfers between devices: 64.6 us -> none  [cross(): totals = lax.psum(buffer, 'tile')]
    all_gather x1 -> x0, blocking collectives: 31.4 us -> none  [gathered_edges(): lax.all_gather(jnp.stack(pieces)[None], 'tile', axis=0, tiled=True)]
    pallas_call x0 -> x1, Pallas kernels: none -> 29.2 us  [local(): pl.pallas_call(functools.partial(kernel, panels, tiles, sub_rows), out_sh...]
    ppermute x8 -> x0, starting transfers between devices: 24.6 us -> none  [passed_along(): return lax.ppermute(block, axis, route)]
    ppermute x8 -> x0, waiting for transfers between devices: 10.6 us -> none  [passed_along(): return lax.ppermute(block, axis, route)]
    all_to_all x2 -> x0, starting transfers between devices: 7.11 us -> none  [cross(): lax.all_to_all(outgoing_of(totals, slot_facts), 'panel', split_axis=0, co...]
    scatter-add x11 -> x0, other arithmetic: 3.88 us -> none  [the longest x8 3.24 us: intersection_add(): summed = summed.at[row_shift:row_shift + block_rows, :, col_shift:col_shi...]
    another operation x11 -> x0, local copies, waits for them, and re-layouts: 3.34 us -> none
  transfers between devices with their start and end apart: 11 -> 0, of which waited for: 5 -> 0; matrix products, arithmetic and copies ran while one was open for 7% -> 0% of each run, Pallas kernels for 0% -> 0%
where the time goes in v1:
time: 33.8 us; the launch traced here: 33.3 us
  Pallas kernels  29.2 us (86%)
  local copies, waits for them, and re-layouts  4.11 us (12%)
    pallas_call x1, Pallas kernels, local(): pl.pallas_call(functools.partial(kernel, panels, tiles, sub_rows), out_sh...  29.2 us
    unnamed x2, local copies, waits for them, and re-layouts  2.86 us
    broadcast_in_dim x1, local copies, waits for them, and re-layouts, local(): blend_weight[None]  1.25 us

profile of v1, /device:TPU:0, one launch (start us, length us, event | category | flops | bytes accessed | tf_op | source)
XLA Modules:
  0.0 33.3 jit_solution(13375451453006011765)
XLA Ops:
  0.0 1.3 %broadcast_in_dim.6.blend = f32[1,576]{1,0:T(1,128)} reshape(f32[576]{0:T(1024)} %param.6) | data formatting | bytes 4608 | tf_op jit(solution)/shard_map/broadcast_in_dim | solution.py:327
  1.3 1.4 %copy.5.seam = s32[4,4,3]{2,1,0:T(4,128)} copy(s32[4,4,3]{1,0,2:T(4,128)} %param.7) | data formatting | bytes 384 | tf_op args[3]
  2.6 29.2 %shard_map.46 = f32[16,8,128]{2,1,0:T(8,128)} custom-call(s32[4,4,3]{2,1,0:T(4,128)} %copy.5.seam, f32[16,8,128]{2,1,0:T(8,128)} %bitcast.5, bf16[2,576,576]{2,1,0:T(8,128)(2,1)} %bitcast.3, f32[1,576]{1,0:T(1,128)} %broadcast_in_dim.6.blend), custom_call_target="tpu_custom_call" | custom-call | tf_op jit(solution)/shard_map/pallas_call | solution.py:299
  31.8 1.5 %copy.7 = f32[1,1,16,8,128]{4,3,2,1,0:T(8,128)} copy(f32[1,1,16,8,128]{4,3,2,1,0:T(8,128)} %bitcast.4) | data formatting | bytes 131072

commit v2 on v1

v2 whole, which is shorter than its diff:
```python
import functools

import jax
import jax.numpy as jnp
from jax import lax
from jax.experimental import pallas as pl
from jax.experimental.pallas import tpu as pltpu
from jax.sharding import PartitionSpec as P

TILE_ROWS = 2
SUB = 8
CELL = SUB * SUB
MESH = pl.DeviceIdType.MESH
SLOTS = 4
UNROLLED = 8
BF = jnp.bfloat16
F32 = jnp.float32


def repeat(count, body):
    if count <= UNROLLED:
        for step in range(count):
            body(step)
    else:
        pl.loop(0, count)(body)


def wrapped(index, size):
    return lax.rem(index + size, size)


def pick(options, index):
    out = options[-1]
    for place in range(len(options) - 2, -1, -1):
        out = jnp.where(index == place, options[place], out)
    return out


def kernel(
    panels, tiles, sub_rows,
    seam_in, residual, inverse, blend, out,
    held, shared, window_out, window_in, ghost_out, ghost_in, part_out, part_in,
    ext, spread, weight, seam, inv_sem, seam_sem,
    tile_send, tile_recv, win_send, win_recv, gho_send, gho_recv, par_send, par_recv,
):
    cols = tiles // TILE_ROWS
    side = cols
    depth = sub_rows + 2
    panel, tile = lax.axis_index("panel"), lax.axis_index("tile")
    row, col = lax.div(tile, cols), lax.rem(tile, cols)

    seam_copy = pltpu.make_async_copy(seam_in, seam, seam_sem.at[0])
    seam_copy.start()
    shift = jnp.where(row == 0, 1, 0)
    span = sub_rows + 1
    wide = max(3, span)

    def on_edge(edge, at_row, at_col):
        return pick([at_col == 0, at_row == 0, at_col == cols - 1, at_row == TILE_ROWS - 1], edge)

    def live_edge(of_panel, at_row, at_col):
        across = seam[of_panel, 0, 0] >= 0
        edge = jnp.where(across, jnp.where(at_col == 0, 0, 2), jnp.where(at_row == 0, 1, 3))
        return edge, on_edge(edge, at_row, at_col)

    def window_start(edge):
        return jnp.where(lax.rem(edge, 2) == 0, row * sub_rows - 1 + shift, col - 1)

    def window_length(edge):
        return jnp.where(lax.rem(edge, 2) == 0, span, 3)

    def planned(count, work):
        if count > UNROLLED:
            return work
        ready = [work(k) for k in range(count)]
        return lambda k: ready[k]

    barrier = pltpu.get_barrier_semaphore()

    def greet_tile(step):
        pl.semaphore_signal(
            barrier, inc=1, device_id=(panel, wrapped(tile + step + 1, tiles)), device_id_type=MESH
        )

    repeat(tiles - 1, greet_tile)
    for off in range(1, panels):
        pl.semaphore_signal(
            barrier, inc=1, device_id=(wrapped(panel + off, panels), tile), device_id_type=MESH
        )

    def load_inverse(n):
        slot = lax.rem(n, SLOTS) if not isinstance(n, int) else n % SLOTS
        return pltpu.make_async_copy(inverse.at[n], held.at[slot], inv_sem.at[slot])

    for n in range(min(sub_rows, SLOTS)):
        load_inverse(n).start()

    def own_blocks(j):
        block = residual[pl.ds(j * SUB, SUB)].reshape(CELL, -1)
        shared[tile * sub_rows + j] = block.astype(BF)
        shared[tiles * sub_rows + j] = jnp.zeros(block.shape, BF)

    repeat(sub_rows, own_blocks)
    window_in[panel] = jnp.zeros(window_in.shape[1:], BF)
    ghost_in[pl.ds(panel * wide, wide)] = jnp.zeros((wide,) + ghost_in.shape[1:], BF)
    spread[...] = jnp.zeros_like(spread)
    pl.semaphore_wait(barrier, tiles - 1 + panels - 1)

    def tile_copy(step, slot, target):
        return pltpu.make_async_remote_copy(
            src_ref=shared.at[pl.ds(slot * sub_rows, sub_rows)],
            dst_ref=shared.at[pl.ds(slot * sub_rows, sub_rows)],
            send_sem=tile_send.at[step], recv_sem=tile_recv.at[slot],
            device_id=(panel, target), device_id_type=MESH,
        )

    repeat(tiles - 1, lambda s: tile_copy(s, tile, wrapped(tile + s + 1, tiles)).start())

    lanes = residual.shape[-1]
    weight[...] = jnp.transpose(jnp.broadcast_to(blend[...].reshape(1, -1), (lanes, blend.shape[0])))
    seam_copy.wait()
    edge, found = live_edge(panel, row, col)
    neighbour = jnp.maximum(seam[panel, edge, 0], 0)
    facing = lax.rem(edge + 2 + seam[panel, edge, 1], 4)
    reverse = seam[panel, edge, 2]

    def source_cell(ghost):
        i, j = lax.shift_right_logical(ghost, 3), ghost & (SUB - 1)
        d = pick([SUB - 1 - j, SUB - 1 - i, j, i], edge)
        s = jnp.where(lax.rem(edge, 2) == 0, i, j)
        s = jnp.where(reverse > 0, SUB - 1 - s, s)
        across = jnp.where(facing >= 2, SUB - 1 - d, d)
        return jnp.where(lax.rem(facing, 2) == 0, s * SUB + across, across * SUB + s)

    shape = (CELL, CELL)
    first, second = lax.broadcasted_iota(jnp.int32, shape, 0), lax.broadcasted_iota(jnp.int32, shape, 1)
    turn = jnp.where((source_cell(first) == second) & found, 1.0, 0.0).astype(BF)
    turn_back = jnp.where((source_cell(second) == first) & found, 1.0, 0.0).astype(BF)

    def plan_window(off):
        other = wrapped(panel + off, panels)
        its_edge, its_found = live_edge(other, row, col)
        ours = its_found & (seam[other, its_edge, 0] == panel)
        my_edge = lax.rem(its_edge + 2 + seam[other, its_edge, 1], 4)
        flip = seam[other, its_edge, 2]
        start, length = window_start(its_edge), window_length(its_edge)

        def place(k):
            b = start + k
            good = ours & (b >= 0) & (b < side) & (k < length)
            b = jnp.where(flip > 0, side - 1 - b, b)
            at_row = pick([b, 0, b, side - 1], my_edge)
            at_col = pick([0, b, cols - 1, b], my_edge)
            block = (lax.div(at_row, sub_rows) * cols + at_col) * sub_rows + lax.rem(at_row, sub_rows)
            return jnp.where(good, block, tiles * sub_rows)

        return planned(wide, place)

    window_places = [plan_window(off) for off in range(1, panels)]

    def plan_inner(ri):
        places = []
        for ci in range(3):
            at_row, at_col = row * sub_rows + ri - 1, col + ci - 1
            inside = (at_row >= 0) & (at_row < side) & (at_col >= 0) & (at_col < cols)
            at_row = jnp.clip(at_row, 0, side - 1)
            block = (lax.div(at_row, sub_rows) * cols + at_col) * sub_rows + lax.rem(at_row, sub_rows)
            places.append(jnp.where(inside, block, tiles * sub_rows))
        return places

    inner_places = planned(depth, plan_inner)

    low = jnp.where(seam[panel, 0, 0] >= 0, 0, 1)
    seams = []
    for own in (low, low + 2):
        far_edge = lax.rem(own + 2 + seam[panel, own, 1], 4)
        far_start = window_start(far_edge)
        far_end = jnp.where(on_edge(far_edge, row, col), far_start + window_length(far_edge), -1)
        seams.append((seam[panel, own, 0], seam[panel, own, 2], far_start, far_end))

    def plan_part(target):
        at_row, at_col = lax.div(target, cols), lax.rem(target, cols)
        its_edge, its_found = live_edge(panel, at_row, at_col)
        other, flip, far_start, far_end = [
            jnp.where(its_edge < 2, lower, upper) for lower, upper in zip(*seams)
        ]

        def place(j):
            ri, ci = (at_row - row) * sub_rows + j + 1, at_col - col + 1
            near = (ri >= 0) & (ri < depth) & (ci >= 0) & (ci < 3)
            b = jnp.where(low == 0, at_row * sub_rows + j, at_col)
            good = its_found & ((low == 0) | (j == jnp.where(its_edge == 1, 0, sub_rows - 1)))
            b = jnp.where(flip > 0, side - 1 - b, b)
            good = good & (b >= far_start) & (b < far_end)
            return (
                jnp.where(near, ri, depth), jnp.where(near, ci, 0),
                jnp.where(good, other * wide + b - far_start, panel * wide),
            )

        return planned(sub_rows, place)

    part_places = planned(tiles, lambda step: plan_part(wrapped(tile + step, tiles)))

    def tile_arrival(step):
        source = wrapped(tile - step - 1, tiles)
        tile_copy(step, source, source).wait_recv()

    repeat(tiles - 1, tile_arrival)

    def window_copy(off, slot, target):
        return pltpu.make_async_remote_copy(
            src_ref=window_out.at[off - 1], dst_ref=window_in.at[slot],
            send_sem=win_send.at[off - 1], recv_sem=win_recv.at[slot],
            device_id=(target, tile), device_id_type=MESH,
        )

    for off in range(1, panels):
        def fill(k, off=off):
            window_out[off - 1, k] = shared[window_places[off - 1](k)]

        repeat(wide, fill)
        window_copy(off, panel, wrapped(panel + off, panels)).start()

    def inner(ri):
        for ci, place in enumerate(inner_places(ri)):
            ext[ri, :, ci] = shared[place].astype(F32).reshape(SUB, SUB, lanes)

    repeat(depth, inner)

    for off in range(1, panels):
        source = wrapped(panel - off, panels)
        window_copy(off, source, source).wait_recv()

    def outer_side(k):
        block = jnp.dot(turn, window_in[neighbour, k], preferred_element_type=F32)
        block = block.reshape(SUB, SUB, lanes)
        for e, (ri, ci) in enumerate(((k + shift, 0), (0, k), (k + shift, 2), (depth - 1, k))):
            if isinstance(k, int) and k < (3 if e % 2 else span):
                ext[ri, :, ci] += jnp.where(edge == e, block, jnp.zeros_like(block))
            elif not isinstance(k, int) and e % 2 == 0:
                ext[ri, :, ci] += jnp.where(edge == e, block, jnp.zeros_like(block))

    for k in range(3):
        outer_side(k)
    if span > 3:
        repeat(span - 3, lambda k: outer_side(jnp.int32(3) + k))

    def solve(n):
        load_inverse(n).wait()
        slot = n % SLOTS if isinstance(n, int) else lax.rem(n, SLOTS)
        patch = ext[pl.ds(n, 3)].reshape(9 * CELL, lanes).astype(BF)
        solved = jnp.dot(held[slot], patch, preferred_element_type=F32) * weight[...]
        spread[pl.ds(n, 3)] += solved.reshape(3, SUB, 3, SUB, lanes)
        if sub_rows > SLOTS:
            @pl.when(n + SLOTS < sub_rows)
            def _():
                load_inverse(n + SLOTS).start()

    repeat(sub_rows, solve)

    def ghost_copy(off, slot, target):
        return pltpu.make_async_remote_copy(
            src_ref=ghost_out, dst_ref=ghost_in.at[pl.ds(slot * wide, wide)],
            send_sem=gho_send.at[off - 1], recv_sem=gho_recv.at[slot],
            device_id=(target, tile), device_id_type=MESH,
        )

    def ghost(k):
        even = lax.rem(edge, 2) == 0
        ri = jnp.where(even, jnp.minimum(k + shift, depth - 1), jnp.where(edge == 1, 0, depth - 1))
        ci = jnp.where(even, edge, jnp.minimum(k, 2))
        raw = spread[ri, :, ci].reshape(CELL, lanes).astype(BF)
        ghost_out[k] = jnp.dot(turn_back, raw, preferred_element_type=F32).astype(BF)

    repeat(wide, ghost)
    for off in range(1, panels):
        ghost_copy(off, panel, wrapped(panel + off, panels)).start()
    for off in range(1, panels):
        source = wrapped(panel - off, panels)
        ghost_copy(off, source, source).wait_recv()

    def part(step, j):
        ri, ci, place = part_places(step)(j)
        return spread[ri, :, ci].reshape(CELL, lanes) + ghost_in[place].astype(F32)

    def part_copy(step, slot, target):
        return pltpu.make_async_remote_copy(
            src_ref=part_out.at[step], dst_ref=part_in.at[slot],
            send_sem=par_send.at[step], recv_sem=par_recv.at[slot],
            device_id=(panel, target), device_id_type=MESH,
        )

    def send_part(step):
        target = wrapped(tile + step + 1, tiles)

        def one(j):
            part_out[step, j] = part(step + 1, j).astype(BF)

        repeat(sub_rows, one)
        part_copy(step, tile, target).start()

    repeat(tiles - 1, send_part)

    def own_part(j):
        out[pl.ds(j * SUB, SUB)] = part(0, j).reshape(SUB, SUB, lanes)

    repeat(sub_rows, own_part)

    def take_part(step):
        source = wrapped(tile - step - 1, tiles)
        part_copy(step, source, source).wait_recv()

        def one(j):
            here = pl.ds(j * SUB, SUB)
            out[here] += part_in[source, j].astype(F32).reshape(SUB, SUB, lanes)

        repeat(sub_rows, one)

    repeat(tiles - 1, take_part)

    def sent(step):
        tile_copy(step, tile, wrapped(tile + step + 1, tiles)).wait_send()
        part_copy(step, tile, wrapped(tile + step + 1, tiles)).wait_send()

    repeat(tiles - 1, sent)
    for off in range(1, panels):
        window_copy(off, panel, wrapped(panel + off, panels)).wait_send()
        ghost_copy(off, panel, wrapped(panel + off, panels)).wait_send()


def local(panels, tiles, residual, inverse, blend_weight, seam_table):
    height, width, lanes = residual.shape[2:]
    sub_rows = height // SUB
    depth = sub_rows + 2
    wide = max(3, sub_rows + 1)
    cells = blend_weight.shape[0]
    vmem = pl.BlockSpec(memory_space=pltpu.VMEM)
    sem = pltpu.SemaphoreType.DMA
    block = (CELL, lanes)
    out = pl.pallas_call(
        functools.partial(kernel, panels, tiles, sub_rows),
        out_shape=jax.ShapeDtypeStruct((height, width, lanes), F32),
        in_specs=[
            pl.BlockSpec(memory_space=pl.ANY), vmem, pl.BlockSpec(memory_space=pl.ANY), vmem,
        ],
        out_specs=vmem,
        scratch_shapes=[
            pltpu.VMEM((min(sub_rows, SLOTS), cells, cells), BF),
            pltpu.VMEM(((tiles + 1) * sub_rows,) + block, BF),
            pltpu.VMEM((panels - 1, wide) + block, BF),
            pltpu.VMEM((panels, wide) + block, BF),
            pltpu.VMEM((wide,) + block, BF),
            pltpu.VMEM((panels * wide,) + block, BF),
            pltpu.VMEM((tiles - 1, sub_rows) + block, BF),
            pltpu.VMEM((tiles, sub_rows) + block, BF),
            pltpu.VMEM((depth, SUB, 3, SUB, lanes), F32),
            pltpu.VMEM((depth + 1, SUB, 3, SUB, lanes), F32),
            pltpu.VMEM((cells, lanes), F32),
            pltpu.SMEM(seam_table.shape, jnp.int32),
            sem((min(sub_rows, SLOTS),)), sem((1,)),
            sem((tiles - 1,)), sem((tiles,)),
            sem((panels - 1,)), sem((panels,)),
            sem((panels - 1,)), sem((panels,)),
            sem((tiles - 1,)), sem((tiles,)),
        ],
        compiler_params=pltpu.CompilerParams(
            collective_id=0, has_side_effects=True, vmem_limit_bytes=67043328
        ),
    )(seam_table, residual[0, 0], inverse[0, 0], blend_weight)
    return out[None, None]


def solution(mesh):
    spec = P("panel", "tile", None, None, None)
    sizes = dict(mesh.shape)
    return jax.shard_map(
        functools.partial(local, sizes["panel"], sizes["tile"]),
        mesh=mesh,
        in_specs=(spec, spec, P(), P()),
        out_specs=spec,
        check_vma=False,
    )
```

time: 33.8 us -> 31.3 us (0.926)
  local copies, waits for them, and re-layouts: 4.11 us -> 2.86 us
  Pallas kernels: 29.2 us -> 28.2 us
    broadcast_in_dim x1 -> x0, local copies, waits for them, and re-layouts: 1.25 us -> none  [local(): blend_weight[None]]
    pallas_call x1, Pallas kernels: 29.2 us -> 28.2 us  [local(): pl.pallas_call(functools.partial(kernel, panels, tiles, sub_rows), out_sh...]
where the time goes in v2:
time: 31.3 us; the launch traced here: 31 us
  Pallas kernels  28.2 us (90%)
  local copies, waits for them, and re-layouts  2.86 us (9%)
    pallas_call x1, Pallas kernels, local(): pl.pallas_call(functools.partial(kernel, panels, tiles, sub_rows), out_sh...  28.2 us
    unnamed x2, local copies, waits for them, and re-layouts  2.86 us

profile of v2, /device:TPU:0, one launch (start us, length us, event | category | flops | bytes accessed | tf_op | source)
XLA Modules:
  0.0 31.0 jit_solution(8428126271826958191)
XLA Ops:
  0.0 1.4 %copy.5.seam_in = s32[4,4,3]{2,1,0:T(4,128)} copy(s32[4,4,3]{1,0,2:T(4,128)} %param.7) | data formatting | bytes 384 | tf_op args[3]
  1.4 28.2 %shard_map.46 = f32[16,8,128]{2,1,0:T(8,128)} custom-call(s32[4,4,3]{2,1,0:T(4,128)} %copy.5.seam_in, f32[16,8,128]{2,1,0:T(8,128)} %bitcast.5, bf16[2,576,576]{2,1,0:T(8,128)(2,1)} %bitcast.3, f32[576]{0:T(1024)} %blend.1), custom_call_target="tpu_custom_call" | custom-call | tf_op jit(solution)/shard_map/pallas_call | solution.py:340
  29.6 1.5 %copy.7 = f32[1,1,16,8,128]{4,3,2,1,0:T(8,128)} copy(f32[1,1,16,8,128]{4,3,2,1,0:T(8,128)} %bitcast.4) | data formatting | bytes 131072

commit v3 on v2

--- a/solution.py
+++ b/solution.py
@@ -59,7 +59,7 @@
         return pick([at_col == 0, at_row == 0, at_col == cols - 1, at_row == TILE_ROWS - 1], edge)
 
     def live_edge(of_panel, at_row, at_col):
-        across = seam[of_panel, 0, 0] >= 0
+        across = seam[0, of_panel, 0] >= 0
         edge = jnp.where(across, jnp.where(at_col == 0, 0, 2), jnp.where(at_row == 0, 1, 3))
         return edge, on_edge(edge, at_row, at_col)
 
@@ -68,6 +68,9 @@
 
     def window_length(edge):
         return jnp.where(lax.rem(edge, 2) == 0, span, 3)
+
+    def peer(step, way):
+        return wrapped(tile + way * (step + 1), tiles)
 
     def planned(count, work):
         if count > UNROLLED:
@@ -79,7 +82,7 @@
 
     def greet_tile(step):
         pl.semaphore_signal(
-            barrier, inc=1, device_id=(panel, wrapped(tile + step + 1, tiles)), device_id_type=MESH
+            barrier, inc=1, device_id=(panel, peer(step, 1)), device_id_type=MESH
         )
 
     repeat(tiles - 1, greet_tile)
@@ -114,15 +117,15 @@
             device_id=(panel, target), device_id_type=MESH,
         )
 
-    repeat(tiles - 1, lambda s: tile_copy(s, tile, wrapped(tile + s + 1, tiles)).start())
+    repeat(tiles - 1, lambda s: tile_copy(s, tile, peer(s, 1)).start())
 
     lanes = residual.shape[-1]
     weight[...] = jnp.transpose(jnp.broadcast_to(blend[...].reshape(1, -1), (lanes, blend.shape[0])))
     seam_copy.wait()
     edge, found = live_edge(panel, row, col)
-    neighbour = jnp.maximum(seam[panel, edge, 0], 0)
-    facing = lax.rem(edge + 2 + seam[panel, edge, 1], 4)
-    reverse = seam[panel, edge, 2]
+    neighbour = jnp.maximum(seam[0, panel, edge], 0)
+    facing = lax.rem(edge + 2 + seam[1, panel, edge], 4)
+    reverse = seam[2, panel, edge]
 
     def source_cell(ghost):
         i, j = lax.shift_right_logical(ghost, 3), ghost & (SUB - 1)
@@ -140,9 +143,9 @@
     def plan_window(off):
         other = wrapped(panel + off, panels)
         its_edge, its_found = live_edge(other, row, col)
-        ours = its_found & (seam[other, its_edge, 0] == panel)
-        my_edge = lax.rem(its_edge + 2 + seam[other, its_edge, 1], 4)
-        flip = seam[other, its_edge, 2]
+        ours = its_found & (seam[0, other, its_edge] == panel)
+        my_edge = lax.rem(its_edge + 2 + seam[1, other, its_edge], 4)
+        flip = seam[2, other, its_edge]
         start, length = window_start(its_edge), window_length(its_edge)
 
         def place(k):
@@ -170,13 +173,13 @@
 
     inner_places = planned(depth, plan_inner)
 
-    low = jnp.where(seam[panel, 0, 0] >= 0, 0, 1)
+    low = jnp.where(seam[0, panel, 0] >= 0, 0, 1)
     seams = []
     for own in (low, low + 2):
-        far_edge = lax.rem(own + 2 + seam[panel, own, 1], 4)
+        far_edge = lax.rem(own + 2 + seam[1, panel, own], 4)
         far_start = window_start(far_edge)
         far_end = jnp.where(on_edge(far_edge, row, col), far_start + window_length(far_edge), -1)
-        seams.append((seam[panel, own, 0], seam[panel, own, 2], far_start, far_end))
+        seams.append((seam[0, panel, own], seam[2, panel, own], far_start, far_end))
 
     def plan_part(target):
         at_row, at_col = lax.div(target, cols), lax.rem(target, cols)
@@ -199,10 +202,10 @@
 
         return planned(sub_rows, place)
 
-    part_places = planned(tiles, lambda step: plan_part(wrapped(tile + step, tiles)))
+    part_places = planned(tiles, lambda step: plan_part(peer(step, 1)))
 
     def tile_arrival(step):
-        source = wrapped(tile - step - 1, tiles)
+        source = peer(step, -1)
         tile_copy(step, source, source).wait_recv()
 
     repeat(tiles - 1, tile_arrival)
@@ -291,10 +294,10 @@
         )
 
     def send_part(step):
-        target = wrapped(tile + step + 1, tiles)
+        target = peer(step, 1)
 
         def one(j):
-            part_out[step, j] = part(step + 1, j).astype(BF)
+            part_out[step, j] = part(step, j).astype(BF)
 
         repeat(sub_rows, one)
         part_copy(step, tile, target).start()
@@ -302,12 +305,12 @@
     repeat(tiles - 1, send_part)
 
     def own_part(j):
-        out[pl.ds(j * SUB, SUB)] = part(0, j).reshape(SUB, SUB, lanes)
+        out[pl.ds(j * SUB, SUB)] = part(tiles - 1, j).reshape(SUB, SUB, lanes)
 
     repeat(sub_rows, own_part)
 
     def take_part(step):
-        source = wrapped(tile - step - 1, tiles)
+        source = peer(step, -1)
         part_copy(step, source, source).wait_recv()
 
         def one(j):
@@ -319,8 +322,8 @@
     repeat(tiles - 1, take_part)
 
     def sent(step):
-        tile_copy(step, tile, wrapped(tile + step + 1, tiles)).wait_send()
-        part_copy(step, tile, wrapped(tile + step + 1, tiles)).wait_send()
+        tile_copy(step, tile, peer(step, 1)).wait_send()
+        part_copy(step, tile, peer(step, 1)).wait_send()
 
     repeat(tiles - 1, sent)
     for off in range(1, panels):
@@ -337,6 +340,7 @@
     vmem = pl.BlockSpec(memory_space=pltpu.VMEM)
     sem = pltpu.SemaphoreType.DMA
     block = (CELL, lanes)
+    fields = jnp.transpose(seam_table, (2, 0, 1))
     out = pl.pallas_call(
         functools.partial(kernel, panels, tiles, sub_rows),
         out_shape=jax.ShapeDtypeStruct((height, width, lanes), F32),
@@ -356,7 +360,7 @@
             pltpu.VMEM((depth, SUB, 3, SUB, lanes), F32),
             pltpu.VMEM((depth + 1, SUB, 3, SUB, lanes), F32),
             pltpu.VMEM((cells, lanes), F32),
-            pltpu.SMEM(seam_table.shape, jnp.int32),
+            pltpu.SMEM(fields.shape, jnp.int32),
             sem((min(sub_rows, SLOTS),)), sem((1,)),
             sem((tiles - 1,)), sem((tiles,)),
             sem((panels - 1,)), sem((panels,)),
@@ -366,7 +370,7 @@
         compiler_params=pltpu.CompilerParams(
             collective_id=0, has_side_effects=True, vmem_limit_bytes=67043328
         ),
-    )(seam_table, residual[0, 0], inverse[0, 0], blend_weight)
+    )(fields, residual[0, 0], inverse[0, 0], blend_weight)
     return out[None, None]
 
 

time: 31.3 us -> 29.9 us (0.955)
  local copies, waits for them, and re-layouts: 2.86 us -> 1.47 us
    unnamed x2 -> x1, local copies, waits for them, and re-layouts: 2.86 us -> 1.47 us
where the time goes in v3:
time: 29.9 us; the launch traced here: 29.7 us
  Pallas kernels  28.2 us (94%)
  local copies, waits for them, and re-layouts  1.47 us (5%)
    pallas_call x1, Pallas kernels, local(): pl.pallas_call(functools.partial(kernel, panels, tiles, sub_rows), out_sh...  28.2 us
    unnamed x1, local copies, waits for them, and re-layouts  1.47 us

profile of v3, /device:TPU:0, one launch (start us, length us, event | category | flops | bytes accessed | tf_op | source)
XLA Modules:
  0.0 29.7 jit_solution(11773893771269762627)
XLA Ops:
  0.0 28.2 %shard_map.46 = f32[16,8,128]{2,1,0:T(8,128)} custom-call(s32[3,4,4]{2,1,0:T(4,128)} %bitcast.7, f32[16,8,128]{2,1,0:T(8,128)} %bitcast.6, bf16[2,576,576]{2,1,0:T(8,128)(2,1)} %bitcast.4, f32[576]{0:T(1024)} %blend.1), custom_call_target="tpu_custom_call" | custom-call | tf_op jit(solution)/shard_map/pallas_call | solution.py:344
  28.2 1.5 %copy.6 = f32[1,1,16,8,128]{4,3,2,1,0:T(8,128)} copy(f32[1,1,16,8,128]{4,3,2,1,0:T(8,128)} %bitcast.5) | data formatting | bytes 131072

commit v4 on v3

--- a/solution.py
+++ b/solution.py
@@ -42,6 +42,7 @@
     held, shared, window_out, window_in, ghost_out, ghost_in, part_out, part_in,
     ext, spread, weight, seam, inv_sem, seam_sem,
     tile_send, tile_recv, win_send, win_recv, gho_send, gho_recv, par_send, par_recv,
+    rest_in, halo_out, halo_in, rest_send, rest_recv, halo_send, halo_recv,
 ):
     cols = tiles // TILE_ROWS
     side = cols
@@ -72,6 +73,27 @@
     def peer(step, way):
         return wrapped(tile + way * (step + 1), tiles)
 
+    near_tiles = ((0, -1), (0, 1), (1, -1), (1, 0), (1, 1))
+
+    def near(slot, action):
+        other_row, away = near_tiles[slot]
+        at_col = col + away
+        target = jnp.where(row == 0, other_row, 1 - other_row) * cols + at_col
+
+        @pl.when((at_col >= 0) & (at_col < cols))
+        def _():
+            action(target, at_col, near_tiles.index((other_row, -away)))
+
+    def at_side(at_col):
+        return (at_col == 0) | (at_col == cols - 1)
+
+    def rim(at_row):
+        return jnp.where(at_row == 0, 0, sub_rows - 1)
+
+    def either(test, yes, no):
+        pl.when(test)(yes)
+        pl.when(jnp.logical_not(test))(no)
+
     def planned(count, work):
         if count > UNROLLED:
             return work
@@ -107,17 +129,45 @@
     window_in[panel] = jnp.zeros(window_in.shape[1:], BF)
     ghost_in[pl.ds(panel * wide, wide)] = jnp.zeros((wide,) + ghost_in.shape[1:], BF)
     spread[...] = jnp.zeros_like(spread)
+    rest_in[rest_in.shape[0] - 1] = jnp.zeros(rest_in.shape[1:], BF)
     pl.semaphore_wait(barrier, tiles - 1 + panels - 1)
 
-    def tile_copy(step, slot, target):
+    def tile_copy(step, slot, target, whole):
+        at = slot * sub_rows + (0 if whole else rim(lax.div(slot, cols)))
+        here = pl.ds(at, sub_rows if whole else 1)
         return pltpu.make_async_remote_copy(
-            src_ref=shared.at[pl.ds(slot * sub_rows, sub_rows)],
-            dst_ref=shared.at[pl.ds(slot * sub_rows, sub_rows)],
+            src_ref=shared.at[here], dst_ref=shared.at[here],
             send_sem=tile_send.at[step], recv_sem=tile_recv.at[slot],
             device_id=(panel, target), device_id_type=MESH,
         )
 
-    repeat(tiles - 1, lambda s: tile_copy(s, tile, peer(s, 1)).start())
+    def send_tile(step):
+        either(
+            at_side(col),
+            lambda: tile_copy(step, tile, peer(step, 1), True).start(),
+            lambda: tile_copy(step, tile, peer(step, 1), False).start(),
+        )
+
+    repeat(tiles - 1, send_tile)
+
+    def rest_copy(slot, target, there):
+        here = pl.ds(tile * sub_rows + jnp.where(row == 0, 1, 0), sub_rows - 1)
+        return pltpu.make_async_remote_copy(
+            src_ref=shared.at[here], dst_ref=rest_in.at[there],
+            send_sem=rest_send.at[slot], recv_sem=rest_recv.at[there],
+            device_id=(panel, target), device_id_type=MESH,
+        )
+
+    def rests(sending, act):
+        if sub_rows == 1:
+            return
+        for slot in range(len(near_tiles)):
+            def action(target, at_col, there, slot=slot):
+                @pl.when(jnp.logical_not(at_side(col if sending else at_col)))
+                def _():
+                    act(rest_copy(slot, target, there if sending else slot))
+
+            near(slot, action)
 
     lanes = residual.shape[-1]
     weight[...] = jnp.transpose(jnp.broadcast_to(blend[...].reshape(1, -1), (lanes, blend.shape[0])))
@@ -167,8 +217,19 @@
             at_row, at_col = row * sub_rows + ri - 1, col + ci - 1
             inside = (at_row >= 0) & (at_row < side) & (at_col >= 0) & (at_col < cols)
             at_row = jnp.clip(at_row, 0, side - 1)
-            block = (lax.div(at_row, sub_rows) * cols + at_col) * sub_rows + lax.rem(at_row, sub_rows)
-            places.append(jnp.where(inside, block, tiles * sub_rows))
+            tile_row, sub = lax.div(at_row, sub_rows), lax.rem(at_row, sub_rows)
+            block = (tile_row * cols + at_col) * sub_rows + sub
+            away = tile_row != row
+            apart = inside & jnp.logical_not(at_side(at_col)) & (sub != rim(tile_row))
+            if ci == 1:
+                apart = apart & away
+            same_row = near_tiles.index((0, ci - 1)) if ci != 1 else 0
+            slot = jnp.where(away, near_tiles.index((1, ci - 1)), same_row)
+            rest = jnp.clip(sub - jnp.where(tile_row == 0, 1, 0), 0, max(sub_rows - 2, 0))
+            places.append((
+                jnp.where(inside & jnp.logical_not(apart), block, tiles * sub_rows),
+                jnp.where(apart, slot, len(near_tiles)), jnp.where(apart, rest, 0),
+            ))
         return places
 
     inner_places = planned(depth, plan_inner)
@@ -189,16 +250,11 @@
         ]
 
         def place(j):
-            ri, ci = (at_row - row) * sub_rows + j + 1, at_col - col + 1
-            near = (ri >= 0) & (ri < depth) & (ci >= 0) & (ci < 3)
             b = jnp.where(low == 0, at_row * sub_rows + j, at_col)
-            good = its_found & ((low == 0) | (j == jnp.where(its_edge == 1, 0, sub_rows - 1)))
+            good = its_found & ((low == 0) | (j == rim(at_row)))
             b = jnp.where(flip > 0, side - 1 - b, b)
             good = good & (b >= far_start) & (b < far_end)
-            return (
-                jnp.where(near, ri, depth), jnp.where(near, ci, 0),
-                jnp.where(good, other * wide + b - far_start, panel * wide),
-            )
+            return jnp.where(good, other * wide + b - far_start, panel * wide)
 
         return planned(sub_rows, place)
 
@@ -206,7 +262,11 @@
 
     def tile_arrival(step):
         source = peer(step, -1)
-        tile_copy(step, source, source).wait_recv()
+        either(
+            at_side(lax.rem(source, cols)),
+            lambda: tile_copy(step, source, source, True).wait_recv(),
+            lambda: tile_copy(step, source, source, False).wait_recv(),
+        )
 
     repeat(tiles - 1, tile_arrival)
 
@@ -224,9 +284,15 @@
         repeat(wide, fill)
         window_copy(off, panel, wrapped(panel + off, panels)).start()
 
+    rests(True, lambda copy: copy.start())
+    rests(False, lambda copy: copy.wait_recv())
+
     def inner(ri):
-        for ci, place in enumerate(inner_places(ri)):
-            ext[ri, :, ci] = shared[place].astype(F32).reshape(SUB, SUB, lanes)
+        for ci, (place, slot, rest) in enumerate(inner_places(ri)):
+            block = shared[place].astype(F32)
+            if sub_rows > 1:
+                block = block + rest_in[slot, rest].astype(F32)
+            ext[ri, :, ci] = block.reshape(SUB, SUB, lanes)
 
     repeat(depth, inner)
 
@@ -278,17 +344,39 @@
     repeat(wide, ghost)
     for off in range(1, panels):
         ghost_copy(off, panel, wrapped(panel + off, panels)).start()
+
+    def halo_copy(slot, target, there):
+        size = sub_rows if near_tiles[slot][0] == 0 else 1
+        return pltpu.make_async_remote_copy(
+            src_ref=halo_out.at[slot, pl.ds(0, size)], dst_ref=halo_in.at[there, pl.ds(0, size)],
+            send_sem=halo_send.at[slot], recv_sem=halo_recv.at[there],
+            device_id=(panel, target), device_id_type=MESH,
+        )
+
+    for slot, (other_row, away) in enumerate(near_tiles):
+        def send_halo(target, at_col, there, slot=slot, other_row=other_row, away=away):
+            def one(j):
+                ri = jnp.where(row == 0, depth - 1, 0) if other_row else j + 1
+                halo_out[slot, j] = spread[ri, :, away + 1].reshape(CELL, lanes).astype(BF)
+
+            repeat(1 if other_row else sub_rows, one)
+            halo_copy(slot, target, there).start()
+
+        near(slot, send_halo)
+
+    def own_part(j):
+        out[pl.ds(j * SUB, SUB)] = spread[j + 1, :, 1]
+
+    repeat(sub_rows, own_part)
+
     for off in range(1, panels):
         source = wrapped(panel - off, panels)
         ghost_copy(off, source, source).wait_recv()
 
-    def part(step, j):
-        ri, ci, place = part_places(step)(j)
-        return spread[ri, :, ci].reshape(CELL, lanes) + ghost_in[place].astype(F32)
-
-    def part_copy(step, slot, target):
+    def part_copy(step, slot, target, whole):
+        here = pl.ds(0, sub_rows) if whole else pl.ds(rim(lax.div(target, cols)), 1)
         return pltpu.make_async_remote_copy(
-            src_ref=part_out.at[step], dst_ref=part_in.at[slot],
+            src_ref=part_out.at[step, here], dst_ref=part_in.at[slot, here],
             send_sem=par_send.at[step], recv_sem=par_recv.at[slot],
             device_id=(panel, target), device_id_type=MESH,
         )
@@ -297,35 +385,64 @@
         target = peer(step, 1)
 
         def one(j):
-            part_out[step, j] = part(step, j).astype(BF)
+            part_out[step, j] = ghost_in[part_places(step)(j)]
 
         repeat(sub_rows, one)
-        part_copy(step, tile, target).start()
+        either(
+            at_side(lax.rem(target, cols)),
+            lambda: part_copy(step, tile, target, True).start(),
+            lambda: part_copy(step, tile, target, False).start(),
+        )
 
     repeat(tiles - 1, send_part)
 
-    def own_part(j):
-        out[pl.ds(j * SUB, SUB)] = part(tiles - 1, j).reshape(SUB, SUB, lanes)
-
-    repeat(sub_rows, own_part)
+    def add(j, block):
+        out[pl.ds(j * SUB, SUB)] += block.astype(F32).reshape(SUB, SUB, lanes)
+
+    repeat(sub_rows, lambda j: add(j, ghost_in[part_places(tiles - 1)(j)]))
+
+    for slot, (other_row, _) in enumerate(near_tiles):
+        def take_halo(target, at_col, there, slot=slot, other_row=other_row):
+            halo_copy(slot, target, slot).wait_recv()
+            if other_row:
+                add(jnp.where(row == 0, sub_rows - 1, 0), halo_in[slot, 0])
+            else:
+                repeat(sub_rows, lambda j: add(j, halo_in[slot, j]))
+
+        near(slot, take_halo)
 
     def take_part(step):
         source = peer(step, -1)
-        part_copy(step, source, source).wait_recv()
-
-        def one(j):
-            here = pl.ds(j * SUB, SUB)
-            out[here] += part_in[source, j].astype(F32).reshape(SUB, SUB, lanes)
-
-        repeat(sub_rows, one)
+
+        def whole():
+            part_copy(step, source, tile, True).wait_recv()
+            repeat(sub_rows, lambda j: add(j, part_in[source, j]))
+
+        def outermost():
+            part_copy(step, source, tile, False).wait_recv()
+            add(rim(row), part_in[source, rim(row)])
+
+        either(at_side(col), whole, outermost)
 
     repeat(tiles - 1, take_part)
 
     def sent(step):
-        tile_copy(step, tile, peer(step, 1)).wait_send()
-        part_copy(step, tile, peer(step, 1)).wait_send()
+        target = peer(step, 1)
+        either(
+            at_side(col),
+            lambda: tile_copy(step, tile, target, True).wait_send(),
+            lambda: tile_copy(step, tile, target, False).wait_send(),
+        )
+        either(
+            at_side(lax.rem(target, cols)),
+            lambda: part_copy(step, tile, target, True).wait_send(),
+            lambda: part_copy(step, tile, target, False).wait_send(),
+        )
 
     repeat(tiles - 1, sent)
+    rests(True, lambda copy: copy.wait_send())
+    for slot in range(len(near_tiles)):
+        near(slot, lambda target, at_col, there, slot=slot: halo_copy(slot, target, there).wait_send())
     for off in range(1, panels):
         window_copy(off, panel, wrapped(panel + off, panels)).wait_send()
         ghost_copy(off, panel, wrapped(panel + off, panels)).wait_send()
@@ -358,7 +475,7 @@
             pltpu.VMEM((tiles - 1, sub_rows) + block, BF),
             pltpu.VMEM((tiles, sub_rows) + block, BF),
             pltpu.VMEM((depth, SUB, 3, SUB, lanes), F32),
-            pltpu.VMEM((depth + 1, SUB, 3, SUB, lanes), F32),
+            pltpu.VMEM((depth, SUB, 3, SUB, lanes), F32),
             pltpu.VMEM((cells, lanes), F32),
             pltpu.SMEM(fields.shape, jnp.int32),
             sem((min(sub_rows, SLOTS),)), sem((1,)),
@@ -366,6 +483,10 @@
             sem((panels - 1,)), sem((panels,)),
             sem((panels - 1,)), sem((panels,)),
             sem((tiles - 1,)), sem((tiles,)),
+            pltpu.VMEM((6, max(sub_rows - 1, 1)) + block, BF),
+            pltpu.VMEM((5, sub_rows) + block, BF),
+            pltpu.VMEM((5, sub_rows) + block, BF),
+            sem((5,)), sem((5,)), sem((5,)), sem((5,)),
         ],
         compiler_params=pltpu.CompilerParams(
             collective_id=0, has_side_effects=True, vmem_limit_bytes=67043328

time: 29.9 us -> 30.3 us (1.013)
  Pallas kernels: 28.2 us -> 28.6 us
    pallas_call x1, Pallas kernels: 28.2 us -> 28.6 us  [local(): pl.pallas_call(functools.partial(kernel, panels, tiles, sub_rows), out_sh...]
where the time goes in v4:
time: 30.3 us; the launch traced here: 30.1 us
  Pallas kernels  28.6 us (94%)
  local copies, waits for them, and re-layouts  1.47 us (5%)
    pallas_call x1, Pallas kernels, local(): pl.pallas_call(functools.partial(kernel, panels, tiles, sub_rows), out_sh...  28.6 us
    unnamed x1, local copies, waits for them, and re-layouts  1.47 us

profile of v4, /device:TPU:0, one launch (start us, length us, event | category | flops | bytes accessed | tf_op | source)
XLA Modules:
  0.0 30.1 jit_solution(9956959478785978092)
XLA Ops:
  0.0 28.6 %shard_map.46 = f32[16,8,128]{2,1,0:T(8,128)} custom-call(s32[3,4,4]{2,1,0:T(4,128)} %bitcast.7, f32[16,8,128]{2,1,0:T(8,128)} %bitcast.6, bf16[2,576,576]{2,1,0:T(8,128)(2,1)} %bitcast.4, f32[576]{0:T(1024)} %blend.1), custom_call_target="tpu_custom_call" | custom-call | tf_op jit(solution)/shard_map/pallas_call | solution.py:461
  28.6 1.5 %copy.6 = f32[1,1,16,8,128]{4,3,2,1,0:T(8,128)} copy(f32[1,1,16,8,128]{4,3,2,1,0:T(8,128)} %bitcast.5) | data formatting | bytes 131072

commit v5 on v4

--- a/solution.py
+++ b/solution.py
@@ -142,11 +142,7 @@
         )
 
     def send_tile(step):
-        either(
-            at_side(col),
-            lambda: tile_copy(step, tile, peer(step, 1), True).start(),
-            lambda: tile_copy(step, tile, peer(step, 1), False).start(),
-        )
+        tile_copy(step, tile, peer(step, 1), True).start()
 
     repeat(tiles - 1, send_tile)
 
@@ -169,6 +165,7 @@
 
             near(slot, action)
 
+
     lanes = residual.shape[-1]
     weight[...] = jnp.transpose(jnp.broadcast_to(blend[...].reshape(1, -1), (lanes, blend.shape[0])))
     seam_copy.wait()
@@ -217,19 +214,8 @@
             at_row, at_col = row * sub_rows + ri - 1, col + ci - 1
             inside = (at_row >= 0) & (at_row < side) & (at_col >= 0) & (at_col < cols)
             at_row = jnp.clip(at_row, 0, side - 1)
-            tile_row, sub = lax.div(at_row, sub_rows), lax.rem(at_row, sub_rows)
-            block = (tile_row * cols + at_col) * sub_rows + sub
-            away = tile_row != row
-            apart = inside & jnp.logical_not(at_side(at_col)) & (sub != rim(tile_row))
-            if ci == 1:
-                apart = apart & away
-            same_row = near_tiles.index((0, ci - 1)) if ci != 1 else 0
-            slot = jnp.where(away, near_tiles.index((1, ci - 1)), same_row)
-            rest = jnp.clip(sub - jnp.where(tile_row == 0, 1, 0), 0, max(sub_rows - 2, 0))
-            places.append((
-                jnp.where(inside & jnp.logical_not(apart), block, tiles * sub_rows),
-                jnp.where(apart, slot, len(near_tiles)), jnp.where(apart, rest, 0),
-            ))
+            block = (lax.div(at_row, sub_rows) * cols + at_col) * sub_rows + lax.rem(at_row, sub_rows)
+            places.append(jnp.where(inside, block, tiles * sub_rows))
         return places
 
     inner_places = planned(depth, plan_inner)
@@ -262,11 +248,7 @@
 
     def tile_arrival(step):
         source = peer(step, -1)
-        either(
-            at_side(lax.rem(source, cols)),
-            lambda: tile_copy(step, source, source, True).wait_recv(),
-            lambda: tile_copy(step, source, source, False).wait_recv(),
-        )
+        tile_copy(step, source, source, True).wait_recv()
 
     repeat(tiles - 1, tile_arrival)
 
@@ -284,15 +266,10 @@
         repeat(wide, fill)
         window_copy(off, panel, wrapped(panel + off, panels)).start()
 
-    rests(True, lambda copy: copy.start())
-    rests(False, lambda copy: copy.wait_recv())
 
     def inner(ri):
-        for ci, (place, slot, rest) in enumerate(inner_places(ri)):
-            block = shared[place].astype(F32)
-            if sub_rows > 1:
-                block = block + rest_in[slot, rest].astype(F32)
-            ext[ri, :, ci] = block.reshape(SUB, SUB, lanes)
+        for ci, place in enumerate(inner_places(ri)):
+            ext[ri, :, ci] = shared[place].astype(F32).reshape(SUB, SUB, lanes)
 
     repeat(depth, inner)
 
@@ -428,11 +405,7 @@
 
     def sent(step):
         target = peer(step, 1)
-        either(
-            at_side(col),
-            lambda: tile_copy(step, tile, target, True).wait_send(),
-            lambda: tile_copy(step, tile, target, False).wait_send(),
-        )
+        tile_copy(step, tile, target, True).wait_send()
         either(
             at_side(lax.rem(target, cols)),
             lambda: part_copy(step, tile, target, True).wait_send(),
@@ -440,7 +413,6 @@
         )
 
     repeat(tiles - 1, sent)
-    rests(True, lambda copy: copy.wait_send())
     for slot in range(len(near_tiles)):
         near(slot, lambda target, at_col, there, slot=slot: halo_copy(slot, target, there).wait_send())
     for off in range(1, panels):

time: 30.3 us -> 29.8 us (0.983)
  Pallas kernels: 28.6 us -> 28.1 us
    pallas_call x1, Pallas kernels: 28.6 us -> 28.1 us  [local(): pl.pallas_call(functools.partial(kernel, panels, tiles, sub_rows), out_sh...]
where the time goes in v5:
time: 29.8 us; the launch traced here: 29.6 us
  Pallas kernels  28.1 us (94%)
  local copies, waits for them, and re-layouts  1.47 us (5%)
    pallas_call x1, Pallas kernels, local(): pl.pallas_call(functools.partial(kernel, panels, tiles, sub_rows), out_sh...  28.1 us
    unnamed x1, local copies, waits for them, and re-layouts  1.47 us

profile of v5, /device:TPU:0, one launch (start us, length us, event | category | flops | bytes accessed | tf_op | source)
XLA Modules:
  0.0 29.6 jit_solution(13654942561595416487)
XLA Ops:
  0.0 28.1 %shard_map.46 = f32[16,8,128]{2,1,0:T(8,128)} custom-call(s32[3,4,4]{2,1,0:T(4,128)} %bitcast.7, f32[16,8,128]{2,1,0:T(8,128)} %bitcast.6, bf16[2,576,576]{2,1,0:T(8,128)(2,1)} %bitcast.4, f32[576]{0:T(1024)} %blend.1), custom_call_target="tpu_custom_call" | custom-call | tf_op jit(solution)/shard_map/pallas_call | solution.py:433
  28.1 1.5 %copy.6 = f32[1,1,16,8,128]{4,3,2,1,0:T(8,128)} copy(f32[1,1,16,8,128]{4,3,2,1,0:T(8,128)} %bitcast.5) | data formatting | bytes 131072
